TPU v7x, 8 devices: a whole 2x2x1 slice. The times are simulated.
8 devices in a mesh: dp: 2 (over y, z), ep: 4 (over x, core).
Axes of the slice: x: 2, y: 2, z: 1, core: 2. Of those that a mesh axis runs over, the one named last changes fastest.
Arguments:
- x: bfloat16 [2, 4, 512, 4096], P('dp', 'ep'), parts along dimension 0
- expert: int32 [2, 4, 512, 2], P('dp', 'ep'), parts along dimension 0
- slot: int32 [2, 4, 512, 2], P('dp', 'ep'), parts along dimension 0
- gate: float32 [2, 4, 512, 2], P('dp', 'ep'), parts along dimension 0
- w_gate: bfloat16 [16, 4096, 6400], P('ep')
- w_up: bfloat16 [16, 4096, 6400], P('ep')
- w_down: bfloat16 [16, 6400, 4096], P('ep')
Outputs:
- y: bfloat16 [2, 4, 512, 4096], P('dp', 'ep'), parts along dimension 0
There are 2 independent parts. A program takes and returns all parts, laid end to end along the dimension named above; an argument that names none is the same for every part.
All inputs are finite; a program needn't handle non-finite values.
Results may differ from a plain program's by a relative error of at most 0.009.
Values are sent between devices in bfloat16 or wider.
A program may use at most 2 GiB of HBM per device.

v0:
```python
import jax
import jax.numpy as jnp
from jax import lax
from jax.sharding import NamedSharding, PartitionSpec as P


def einsum(form, a, b):
    return jnp.einsum(form, a.astype(jnp.float32), b.astype(jnp.float32))


def solution(mesh):
    def placed(v, *spec):
        return lax.with_sharding_constraint(v, NamedSharding(mesh, P(*spec)))

    def step(x, expert, slot, gate, w_gate, w_up, w_down):
        experts, (tokens, top) = w_gate.shape[0], expert.shape[2:]
        slots = 5 * tokens * top // (4 * experts)
        to_expert = jax.nn.one_hot(expert, experts, dtype=jnp.bfloat16)
        to_slot = jax.nn.one_hot(slot, slots, dtype=jnp.bfloat16)
        weighted = to_expert * gate[..., None].astype(jnp.bfloat16)
        dispatch = einsum("abtke,abtkc->abtec", to_expert, to_slot).astype(jnp.bfloat16)
        combine = einsum("abtke,abtkc->abtec", weighted, to_slot).astype(jnp.bfloat16)
        z = einsum("abtec,abtd->aebcd", dispatch, x).astype(jnp.bfloat16)
        z = placed(z, "dp", None, "ep", None, None)
        z = placed(z, "dp", "ep", None, None, None)
        h = jax.nn.silu(einsum("aebcd,edf->aebcf", z, w_gate))
        h = (h * einsum("aebcd,edf->aebcf", z, w_up)).astype(jnp.bfloat16)
        out = einsum("aebcf,efd->aebcd", h, w_down).astype(jnp.bfloat16)
        out = placed(out, "dp", "ep", None, None, None)
        out = placed(out, "dp", None, "ep", None, None)
        y = einsum("abtec,aebcd->abtd", combine, out)
        return y.astype(jnp.bfloat16)

    return step
```

profile of v0, /device:TPU:0, one launch (start us, length us, event | category | flops | bytes accessed | tf_op | source)
XLA Modules:
  0.0 546.8 jit_solution(2873811694338058513)
XLA Ops:
  0.0 0.8 copy.11
  0.8 0.0 copy-start.1
  0.8 0.9 copy.9
  1.7 0.0 copy-start.3
  1.7 0.0 copy-start
  1.7 4.0 convolution_convert_fusion.1
  5.7 0.0 copy-done
  5.7 6.5 %convolution_convert_fusion = bf16[16,80,4096]{2,1,0:T(8,128)(2,1)S(1)} fusion(bf16[1,1,512,4096]{3,2,1,0:T(8,128)(2,1)S(1)} %copy-done, bf16[512,16,80]{2,1,0:T(8,128)(2,1)S(1)} %convolution_convert_fusion.1), kind=kOutput, calls=%fused_computation.21 | convolution fusion | flops 5373952000 | bytes 15990784 | tf_op jit(solution)/abtec,abtd->aebcd/dot_general | solution.py:8
  12.2 0.0 copy-done.1
  12.2 0.0 copy-done.3
  12.2 120.6 %all-to-all.4 = bf16[1,4,4,1,80,4096]{5,4,2,3,0,1:T(8,128)(2,1)} all-to-all(bf16[1,4,4,1,80,4096]{5,4,2,3,0,1:T(8,128)(2,1)S(1)} %bitcast.124), channel_id=1, replica_groups=mesh['dp'=2,'ep'=4] {'ep'}, dimensions={1} | all-to-all | bytes 20971520 | tf_op jit(solution)/sharding_constraint;jit(solution)/sharding_constraint | solution.py:13
  132.9 89.6 %fusion.2 = f32[4,4,80,6400]{3,2,1,0:T(8,128)} fusion(bf16[4,4096,6400]{2,1,0:T(8,128)(2,1)} %param.5, bf16[1,4,4,1,80,4096]{5,4,2,3,0,1:T(8,128)(2,1)} %all-to-all.4), kind=kOutput, calls=%fused_computation.2 | convolution fusion | flops 67108864000 | bytes 252968960 | tf_op jit(solution)/aebcd,edf->aebcf/dot_general | solution.py:8
  222.5 92.6 %fusion.60 = bf16[4,4,80,6400]{3,2,1,0:T(8,128)(2,1)} fusion(f32[4,4,80,6400]{3,2,1,0:T(8,128)} %fusion.2, bf16[4,4096,6400]{2,1,0:T(8,128)(2,1)} %param.4, bf16[1,4,4,1,80,4096]{5,4,2,3,0,1:T(8,128)(2,1)} %all-to-all.4), kind=kOutput, calls=%fused_computation.13.clone.clone.clone.1 | convolution fusion | flops 67158016000 | bytes 269352960 | tf_op jit(solution)/aebcd,edf->aebcf/dot_general | solution.py:8
  315.0 88.2 %convert_bitcast_fusion = bf16[1,4,4,1,80,4096]{5,4,2,1,3,0:T(8,128)(2,1)} fusion(bf16[4,6400,4096]{2,1,0:T(8,128)(2,1)} %param.6, bf16[4,4,80,6400]{3,2,1,0:T(8,128)(2,1)} %fusion.60), kind=kOutput, calls=%fused_computation.17 | convolution fusion | flops 67114106880 | bytes 236584960 | tf_op jit(solution)/aebcf,efd->aebcd/dot_general | solution.py:8
  403.3 9.6 %copy.15 = bf16[1,4,4,1,80,4096]{5,4,1,3,0,2:T(8,128)(2,1)} copy(bf16[1,4,4,1,80,4096]{5,4,2,1,3,0:T(8,128)(2,1)} %convert_bitcast_fusion) | data formatting | bytes 20971520 | tf_op jit(solution)/sharding_constraint;jit(solution)/sharding_constraint | solution.py:13
  412.9 0.0 copy-start.2
  412.9 6.1 %all-to-all-start.1 = ((bf16[1,4,4,1,80,4096]{5,4,1,3,0,2:T(8,128)(2,1)}), bf16[1,4,4,1,80,4096]{5,4,1,3,0,2:T(8,128)(2,1)}, u32[]{:S(2)}, u32[]{:S(2)}) async-start(bf16[1,4,4,1,80,4096]{5,4,1,3,0,2:T(8,128)(2,1)} %copy.15), calls=%async_computation.1 | async-start | bytes 20971520 | tf_op jit(solution)/sharding_constraint;jit(solution)/sharding_constraint | solution.py:13
  419.0 0.0 copy-done.5
  419.0 0.2 copy.10
  419.2 0.0 copy-done.2
  419.2 0.0 copy-done.4
  419.2 4.8 convolution_convert_fusion.2
  424.1 110.2 %all-to-all-done.1 = bf16[1,4,4,1,80,4096]{5,4,1,3,0,2:T(8,128)(2,1)} async-done(((bf16[1,4,4,1,80,4096]{5,4,1,3,0,2:T(8,128)(2,1)}), bf16[1,4,4,1,80,4096]{5,4,1,3,0,2:T(8,128)(2,1)}, u32[]{:S(2)}, u32[]{:S(2)}) %all-to-all-start.1) | async-done | bytes 10485792 | tf_op jit(solution)/sharding_constraint;jit(solution)/sharding_constraint | solution.py:13
  534.3 12.5 %fusion.32 = bf16[1,1,512,4096]{3,2,1,0:T(8,128)(2,1)} fusion(bf16[16,80,4096]{2,1,0:T(8,128)(2,1)} %bitcast.25, bf16[512,16,80]{2,1,0:T(8,128)(2,1)S(1)} %convolution_convert_fusion.2), kind=kOutput, calls=%fused_computation.22 | convolution fusion | flops 5370806272 | bytes 15990784 | tf_op jit(solution)/abtec,aebcd->abtd/dot_general | solution.py:8
  (3 shorter events, 0.0 us)
Async XLA Ops:
  0.8 11.4 %copy-start.1 = (s32[512,2]{1,0:T(8,128)}, s32[512,2]{1,0:T(8,128)S(1)}, u32[]{:S(2)}) copy-start(s32[512,2]{1,0:T(8,128)S(1)} %copy.11) | copy-start | bytes 12292
  1.7 10.5 %copy-start.3 = (s32[512,2]{1,0:T(8,128)}, s32[512,2]{1,0:T(8,128)S(1)}, u32[]{:S(2)}) copy-start(s32[512,2]{1,0:T(8,128)S(1)} %copy.9) | copy-start | bytes 12292
  1.7 4.0 copy-start
  412.9 6.2 %copy-start.5 = (f32[1,1,512,2]{2,3,1,0:T(2,128)S(1)}, f32[1,1,512,2]{2,3,1,0:T(2,128)}, u32[]{:S(2)}) copy-start(f32[1,1,512,2]{2,3,1,0:T(2,128)} %param.1) | copy-start | bytes 12292
  412.9 6.4 %copy-start.2 = (s32[512,2]{1,0:T(8,128)S(1)}, s32[512,2]{1,0:T(8,128)}, u32[]{:S(2)}) copy-start(s32[512,2]{1,0:T(8,128)} %copy-done.1) | copy-start | bytes 12292
  412.9 6.4 %copy-start.4 = (s32[512,2]{1,0:T(8,128)S(1)}, s32[512,2]{1,0:T(8,128)}, u32[]{:S(2)}) copy-start(s32[512,2]{1,0:T(8,128)} %copy-done.3) | copy-start | bytes 12292
  412.9 121.4 %all-to-all-start.1 = ((bf16[1,4,4,1,80,4096]{5,4,1,3,0,2:T(8,128)(2,1)}), bf16[1,4,4,1,80,4096]{5,4,1,3,0,2:T(8,128)(2,1)}, u32[]{:S(2)}, u32[]{:S(2)}) async-start(bf16[1,4,4,1,80,4096]{5,4,1,3,0,2:T(8,128)(2,1)} %copy.15), calls=%async_computation.1 | async-start | bytes 20971520 | tf_op jit(solution)/sharding_constraint;jit(solution)/sharding_constraint | solution.py:13
where the time goes:
time: 547 us
  matrix products  298 us (54%)
  blocking collectives  121 us (22%)
  waiting for transfers between devices  110 us (20%)
  local copies, waits for them, and re-layouts  11.5 us (2%)
  starting transfers between devices  6.15 us (1%)
    dot_general x7, matrix products, einsum(): return jnp.einsum(form, a.astype(jnp.float32), b.astype(jnp.float32))  298 us
    another operation x1, blocking collectives, placed(): return lax.with_sharding_constraint(v, NamedSharding(mesh, P(*spec)))  121 us
    another operation x1, waiting for transfers between devices, placed(): return lax.with_sharding_constraint(v, NamedSharding(mesh, P(*spec)))  110 us
  transfers between devices with their start and end apart: 1, of which 1 were waited for; matrix products, arithmetic and copies ran while one was open for 1% of the time, Pallas kernels for 0%

commit v1 on v0

v1 whole, which is shorter than its diff:
```python
import functools

import jax
import jax.numpy as jnp
from jax import lax
from jax.experimental import pallas as pl
from jax.experimental.pallas import tpu as pltpu
from jax.sharding import PartitionSpec as P

MESH = pl.DeviceIdType.MESH
FT, DT, RING = 256, 512, 4


def einsum(form, a, b):
    return jnp.einsum(form, a.astype(jnp.float32), b.astype(jnp.float32))


def ffn_kernel(s_ref, wg, wu, wd, r_ref, z, h, o, ring, w_sem, z_send, z_recv, z_own, o_send, o_recv, o_own):
    members, experts, slots, d = s_ref.shape
    f = wg.shape[2]
    n1, n2 = f // FT, d // DT
    steps = n1 + n2
    me = lax.axis_index("ep")
    group = lax.axis_index("dp")

    def peer(k):
        return me ^ k

    def rows(i):
        return pl.ds(pl.multiple_of(i * slots, slots), slots)

    def w_issue(g):
        e, s, at = g // steps, lax.rem(g, steps), lax.rem(g, RING)

        @pl.when(s < n1)
        def _():
            c = pl.ds(pl.multiple_of(s * FT, FT), FT)
            for j, w in enumerate((wg, wu)):
                pltpu.make_async_copy(
                    w.at[e, :, c], ring.at[at, pl.ds(0, d), pl.ds(j * FT, FT)], w_sem.at[at, j]
                ).start()

        @pl.when(s >= n1)
        def _():
            c = pl.ds(pl.multiple_of((s - n1) * DT, DT), DT)
            pltpu.make_async_copy(wd.at[e, :, c], ring.at[at], w_sem.at[at, 0]).start()

    def z_copy(e, k):
        return pltpu.make_async_remote_copy(
            s_ref.at[peer(k), e], z.at[e, rows(me)], z_send.at[e, k - 1], z_recv.at[e, k - 1],
            device_id=(group, peer(k)), device_id_type=MESH,
        )

    def z_arrival(e, k):
        return pltpu.make_async_remote_copy(
            s_ref.at[peer(k), e], z.at[e, rows(peer(k))], z_send.at[e, k - 1], z_recv.at[e, k - 1],
            device_id=(group, peer(k)), device_id_type=MESH,
        )

    def z_local(e):
        return pltpu.make_async_copy(s_ref.at[me, e], z.at[e, rows(me)], z_own.at[e])

    def o_copy(e, s, k):
        c = pl.ds(pl.multiple_of(s * DT, DT), DT)
        return pltpu.make_async_remote_copy(
            o.at[lax.rem(e, 2), rows(peer(k)), c], r_ref.at[me, e, :, c], o_send.at[e, s, k - 1],
            o_recv.at[e, s, k - 1], device_id=(group, peer(k)), device_id_type=MESH,
        )

    def o_arrival(e, s, k):
        c = pl.ds(pl.multiple_of(s * DT, DT), DT)
        return pltpu.make_async_remote_copy(
            o.at[lax.rem(e, 2), rows(me), c], r_ref.at[peer(k), e, :, c], o_send.at[e, s, k - 1],
            o_recv.at[e, s, k - 1], device_id=(group, peer(k)), device_id_type=MESH,
        )

    def o_local(e, s):
        c = pl.ds(pl.multiple_of(s * DT, DT), DT)
        return pltpu.make_async_copy(o.at[lax.rem(e, 2), rows(me), c], r_ref.at[me, e, :, c], o_own.at[e, s])

    for g in range(RING - 1):
        w_issue(g)
    barrier = pltpu.get_barrier_semaphore()
    for k in (1, 2, 3):
        pl.semaphore_signal(barrier, inc=1, device_id=(group, peer(k)), device_id_type=MESH)
    pl.semaphore_wait(barrier, 3)
    for e in range(experts):
        for k in (2, 3, 1):
            z_copy(e, k).start()
        z_local(e).start()

    def give_back(e, s):
        for k in (2, 3, 1):
            o_copy(e, s, k).start()
        o_local(e, s).start()

    def given(e):
        def one(s, _):
            for k in (1, 2, 3):
                o_copy(e, s, k).wait_send()
            o_local(e, s).wait()
            return 0

        lax.fori_loop(0, n2, one, 0)

    def expert(e, _):
        for k in (1, 2, 3):
            z_arrival(e, k).wait_recv()
        z_local(e).wait()

        def up(s, _):
            g = e * steps + s
            at = lax.rem(g, RING)

            @pl.when(g + RING - 1 < experts * steps)
            def _():
                w_issue(g + RING - 1)

            for j, w in enumerate((wg, wu)):
                pltpu.make_async_copy(
                    w.at[0, :, pl.ds(0, FT)], ring.at[at, pl.ds(0, d), pl.ds(j * FT, FT)], w_sem.at[at, j]
                ).wait()
            both = jnp.dot(z[e], ring[at, :d, :], preferred_element_type=jnp.float32)
            a, b = both[:, :FT], both[:, FT:]
            h[:, pl.ds(pl.multiple_of(s * FT, FT), FT)] = (jax.nn.silu(a) * b).astype(h.dtype)
            return 0

        lax.fori_loop(0, n1, up, 0)

        @pl.when(e >= 2)
        def _():
            given(e - 2)

        def down(s, _):
            g = e * steps + n1 + s
            at = lax.rem(g, RING)

            @pl.when(g + RING - 1 < experts * steps)
            def _():
                w_issue(g + RING - 1)

            pltpu.make_async_copy(wd.at[0, :, pl.ds(0, DT)], ring.at[at], w_sem.at[at, 0]).wait()

            @pl.when(s >= 1)
            def _():
                give_back(e, s - 1)

            c = pl.ds(pl.multiple_of(s * DT, DT), DT)
            o[lax.rem(e, 2), :, c] = jnp.dot(h[...], ring[at], preferred_element_type=jnp.float32).astype(o.dtype)
            return 0

        lax.fori_loop(0, n2, down, 0)
        give_back(e, n2 - 1)
        return 0

    lax.fori_loop(0, experts, expert, 0)
    given(experts - 2)
    given(experts - 1)

    def last(e, _):
        for k in (1, 2, 3):
            z_copy(e, k).wait_send()

        def one(s, _):
            for k in (1, 2, 3):
                o_arrival(e, s, k).wait_recv()
            return 0

        return lax.fori_loop(0, n2, one, 0)

    lax.fori_loop(0, experts, last, 0)


def moe(s, wg, wu, wd):
    members, experts, slots, d = s.shape
    f = wg.shape[2]
    n2 = d // DT
    dma, rows = pltpu.SemaphoreType.DMA, members * slots
    return pl.pallas_call(
        ffn_kernel,
        out_shape=jax.ShapeDtypeStruct(s.shape, s.dtype),
        in_specs=[pl.BlockSpec(memory_space=pl.ANY)] * 4,
        out_specs=pl.BlockSpec(memory_space=pl.ANY),
        scratch_shapes=[
            pltpu.VMEM((experts, rows, d), s.dtype),
            pltpu.VMEM((rows, f), s.dtype),
            pltpu.VMEM((2, rows, d), s.dtype),
            pltpu.VMEM((RING, f, 2 * FT), s.dtype),
            dma((RING, 2)),
            dma((experts, 3)),
            dma((experts, 3)),
            dma((experts,)),
            dma((experts, n2, 3)),
            dma((experts, n2, 3)),
            dma((experts, n2)),
        ],
        compiler_params=pltpu.CompilerParams(
            collective_id=0, has_side_effects=True, vmem_limit_bytes=60 * 2**20
        ),
    )(s, wg, wu, wd)


def solution(mesh):
    members = mesh.shape["ep"]

    def step(x, expert, slot, gate, w_gate, w_up, w_down):
        x, expert, slot, gate = x[0, 0], expert[0, 0], slot[0, 0], gate[0, 0]
        (tokens, top), experts, d = expert.shape, members * w_gate.shape[0], x.shape[1]
        slots = 5 * tokens * top // (4 * experts)
        to_expert = jax.nn.one_hot(expert, experts, dtype=jnp.bfloat16)
        to_slot = jax.nn.one_hot(slot, slots, dtype=jnp.bfloat16)
        weighted = to_expert * gate[..., None].astype(jnp.bfloat16)
        dispatch = einsum("tke,tkc->tec", to_expert, to_slot).astype(jnp.bfloat16)
        combine = einsum("tke,tkc->tec", weighted, to_slot).astype(jnp.bfloat16)
        s = einsum("tec,td->ecd", dispatch, x).astype(jnp.bfloat16)
        s = s.reshape(members, experts // members, slots, d)
        r = moe(s, w_gate, w_up, w_down).reshape(experts, slots, d)
        y = einsum("tec,ecd->td", combine, r)
        return y.astype(jnp.bfloat16)[None, None]

    own, weights = P("dp", "ep"), P("ep")
    return jax.shard_map(
        step, mesh=mesh, in_specs=(own, own, own, own, weights, weights, weights), out_specs=own, check_vma=False
    )
```

time: 547 us -> 315 us (0.58)
  Pallas kernels: 0 us -> 279 us
  matrix products: 298 us -> 30.3 us
  blocking collectives: 121 us -> 0 us
  waiting for transfers between devices: 110 us -> 0 us
  starting transfers between devices: 6.15 us -> 0 us
  local copies, waits for them, and re-layouts: 11.5 us -> 5.74 us
    pallas_call x0 -> x1, Pallas kernels: none -> 279 us  [moe(): pl.pallas_call(ffn_kernel, out_shape=jax.ShapeDtypeStruct(s.shape, s.dtyp...]
    dot_general x7 -> x4, matrix products: 298 us -> 30.3 us  [einsum(): return jnp.einsum(form, a.astype(jnp.float32), b.astype(jnp.float32))]
    another operation x1 -> x0, blocking collectives: 121 us -> none  [placed(): return lax.with_sharding_constraint(v, NamedSharding(mesh, P(*spec)))]
    another operation x1 -> x0, waiting for transfers between devices: 110 us -> none  [placed(): return lax.with_sharding_constraint(v, NamedSharding(mesh, P(*spec)))]
    another operation x1 -> x0, local copies, waits for them, and re-layouts: 9.59 us -> none  [placed(): return lax.with_sharding_constraint(v, NamedSharding(mesh, P(*spec)))]
    another operation x1 -> x0, starting transfers between devices: 6.15 us -> none  [placed(): return lax.with_sharding_constraint(v, NamedSharding(mesh, P(*spec)))]
  transfers between devices with their start and end apart: 1 -> 0, of which waited for: 1 -> 0; matrix products, arithmetic and copies ran while one was open for 1% -> 0% of each run, Pallas kernels for 0% -> 0%
where the time goes in v1:
time: 315 us
  Pallas kernels  279 us (89%)
  matrix products  30.3 us (10%)
  local copies, waits for them, and re-layouts  5.74 us (2%)
    pallas_call x1, Pallas kernels, moe(): pl.pallas_call(ffn_kernel, out_shape=jax.ShapeDtypeStruct(s.shape, s.dtyp...  279 us
    dot_general x4, matrix products, einsum(): return jnp.einsum(form, a.astype(jnp.float32), b.astype(jnp.float32))  30.3 us

profile of v1, /device:TPU:0, one launch (start us, length us, event | category | flops | bytes accessed | tf_op | source)
XLA Modules:
  0.0 314.9 jit_solution(8158520661981142718)
XLA Ops:
  0.0 0.8 copy.10
  0.8 0.0 copy-start
  0.8 0.9 copy.8
  1.7 0.0 copy-done
  1.7 0.0 copy-start.2
  1.7 0.7 copy-done.2
  2.4 4.0 %fusion.4 = bf16[512,16,80]{2,1,0:T(8,128)(2,1)S(1)} fusion(s32[512,2]{1,0:T(8,128)S(1)} %copy.10, s32[512,2]{1,0:T(8,128)S(1)} %copy.8), kind=kOutput, calls=%fused_computation.7 | convolution fusion | flops 2719744 | bytes 1318912 | tf_op jit(solution)/shard_map/tke,tkc->tec/dot_general | solution.py:15
  6.4 1.6 copy.12
  8.0 10.2 %convolution_convert_fusion = bf16[16,80,4096]{2,1,0:T(8,128)(2,1)} fusion(bf16[1,1,512,4096]{3,2,1,0:T(8,128)(2,1)} %param.7, bf16[512,16,80]{0,2,1:T(8,128)(2,1)S(1)} %copy.12), kind=kOutput, calls=%fused_computation.1 | convolution fusion | flops 5373952000 | bytes 15990784 | tf_op jit(solution)/shard_map/tec,td->ecd/dot_general | solution.py:15
  18.2 0.0 copy-start.4
  18.2 0.0 copy-start.1
  18.2 0.0 copy-start.3
  18.2 278.8 %shard_map.73 = bf16[4,4,80,4096]{3,2,1,0:T(8,128)(2,1)} custom-call(bf16[4,4,80,4096]{3,2,1,0:T(8,128)(2,1)} %bitcast.21, bf16[4,4096,6400]{2,1,0:T(8,128)(2,1)} %wg.1, bf16[4,4096,6400]{2,1,0:T(8,128)(2,1)} %wu.1, bf16[4,6400,4096]{2,1,0:T(8,128)(2,1)} %wd.1), custom_call_target="tpu_custom_call" | custom-call | tf_op jit(solution)/shard_map/pallas_call | solution.py:179
  297.0 0.0 copy-done.4
  297.0 0.2 copy.9
  297.2 0.0 copy-done.1
  297.2 0.0 copy-done.3
  297.2 4.8 %fusion.5 = bf16[512,16,80]{2,1,0:T(8,128)(2,1)S(1)} fusion(s32[512,2]{1,0:T(8,128)S(1)} %copy-done.1, s32[512,2]{1,0:T(8,128)S(1)} %copy-done.3, bf16[512,2]{1,0:T(8,128)(2,1)S(1)} %copy.9), kind=kOutput, calls=%fused_computation.8 | convolution fusion | flops 2736128 | bytes 1320960 | tf_op jit(solution)/shard_map/tke,tkc->tec/dot_general | solution.py:15
  302.1 1.6 copy.11
  303.7 11.2 %fusion = bf16[1,1,512,4096]{3,2,1,0:T(8,128)(2,1)} fusion(bf16[16,80,4096]{2,1,0:T(8,128)(2,1)} %bitcast.20, bf16[512,16,80]{0,2,1:T(8,128)(2,1)S(1)} %copy.11), kind=kOutput, calls=%fused_computation.2 | convolution fusion | flops 5370806272 | bytes 15990784 | tf_op jit(solution)/shard_map/tec,ecd->td/dot_general | solution.py:15
  (1 shorter events, 0.0 us)
Async XLA Ops:
  0.8 0.9 copy-start
  1.7 0.7 copy-start.2
  18.2 278.8 %copy-start.4 = (f32[1,1,512,2]{2,3,1,0:T(2,128)S(1)}, f32[1,1,512,2]{2,3,1,0:T(2,128)}, u32[]{:S(2)}) copy-start(f32[1,1,512,2]{2,3,1,0:T(2,128)} %param.10) | copy-start | bytes 12292
  18.2 279.0 %copy-start.1 = (s32[512,2]{1,0:T(8,128)S(1)}, s32[512,2]{1,0:T(8,128)}, u32[]{:S(2)}) copy-start(s32[512,2]{1,0:T(8,128)} %copy-done) | copy-start | bytes 12292
  18.2 279.0 %copy-start.3 = (s32[512,2]{1,0:T(8,128)S(1)}, s32[512,2]{1,0:T(8,128)}, u32[]{:S(2)}) copy-start(s32[512,2]{1,0:T(8,128)} %copy-done.2) | copy-start | bytes 12292

commit v2 on v1

v2 whole, which is shorter than its diff:
```python
import functools

import jax
import jax.numpy as jnp
from jax import lax
from jax.experimental import pallas as pl
from jax.experimental.pallas import tpu as pltpu
from jax.sharding import PartitionSpec as P

MESH = pl.DeviceIdType.MESH
FT, DT, RING, PAIR = 256, 512, 5, 2
AHEAD = RING - PAIR


def cell_of(expert_ref, slot_ref, slots):
    slot = slot_ref[...]
    return jnp.where(slot < slots, expert_ref[...] * slots + slot, -1)


def ffn_kernel(
    expert_ref, slot_ref, x_ref, wg, wu, wd, r_ref, sent, z, h, o, ring,
    x_sem, w_sem, z_send, z_recv, o_send, o_recv, o_own,
):
    experts, rows_z, d = z.shape
    members = r_ref.shape[0]
    slots = rows_z // members
    tokens, f = x_ref.shape[0], wg.shape[2]
    n1, n2 = f // FT, d // DT
    steps, total, back = n1 + n2, experts * (n1 + n2), n2 // PAIR
    me, group = lax.axis_index("ep"), lax.axis_index("dp")

    def peer(k):
        return me ^ k

    def rows(i):
        return pl.ds(pl.multiple_of(i * slots, slots), slots)

    def x_copy(j):
        return pltpu.make_async_copy(
            x_ref.at[:, pl.ds(j * DT, DT)], ring.at[RING - 1, pl.ds(j * tokens, tokens)], x_sem.at[j]
        )

    def w_issue(g):
        e, s, at = g // steps, lax.rem(g, steps), lax.rem(g, RING)

        @pl.when((s < n1) & (g < total))
        def _():
            c = pl.ds(pl.multiple_of(s * FT, FT), FT)
            for j, w in enumerate((wg, wu)):
                pltpu.make_async_copy(
                    w.at[e, :, c], ring.at[at, pl.ds(0, d), pl.ds(j * FT, FT)], w_sem.at[at, j]
                ).start()

        @pl.when((s >= n1) & (g < total))
        def _():
            c = pl.ds(pl.multiple_of((s - n1) * DT, DT), DT)
            pltpu.make_async_copy(wd.at[e, :, c], ring.at[at], w_sem.at[at, 0]).start()

    def z_copy(e, k):
        return pltpu.make_async_remote_copy(
            sent.at[e, pl.ds((k - 1) * slots, slots)], z.at[e, rows(me)], z_send.at[e, k - 1], z_recv.at[e, k - 1],
            device_id=(group, peer(k)), device_id_type=MESH,
        )

    def z_arrival(e, k):
        return pltpu.make_async_remote_copy(
            sent.at[e, pl.ds((k - 1) * slots, slots)], z.at[e, rows(peer(k))], z_send.at[e, k - 1],
            z_recv.at[e, k - 1], device_id=(group, peer(k)), device_id_type=MESH,
        )

    def back_columns(s):
        return pl.ds(pl.multiple_of(s * (PAIR * DT), PAIR * DT), PAIR * DT)

    def o_copy(e, s, k):
        c = back_columns(s)
        return pltpu.make_async_remote_copy(
            o.at[lax.rem(e, 2), rows(peer(k)), c], r_ref.at[me, e, :, c], o_send.at[e, s, k - 1],
            o_recv.at[e, s, k - 1], device_id=(group, peer(k)), device_id_type=MESH,
        )

    def o_arrival(e, s, k):
        c = back_columns(s)
        return pltpu.make_async_remote_copy(
            o.at[lax.rem(e, 2), rows(me), c], r_ref.at[peer(k), e, :, c], o_send.at[e, s, k - 1],
            o_recv.at[e, s, k - 1], device_id=(group, peer(k)), device_id_type=MESH,
        )

    def o_local(e, s):
        c = back_columns(s)
        return pltpu.make_async_copy(o.at[lax.rem(e, 2), rows(me), c], r_ref.at[me, e, :, c], o_own.at[e, s])

    for j in range(n2):
        x_copy(j).start()
    barrier = pltpu.get_barrier_semaphore()
    for k in (1, 2, 3):
        pl.semaphore_signal(barrier, inc=1, device_id=(group, peer(k)), device_id_type=MESH)
    for g in range(AHEAD):
        w_issue(jnp.int32(g))

    cell = cell_of(expert_ref, slot_ref, slots)
    row = lax.broadcasted_iota(jnp.int32, (rows_z, tokens), 0)
    k_of = sum((row >= i * slots).astype(jnp.int32) for i in range(1, members))
    first = (me ^ k_of) * (experts * slots) + row - k_of * slots
    for j in range(n2):
        x_copy(j).wait()
    pl.semaphore_wait(barrier, 3)

    def send(e):
        for k in (2, 3, 1):
            z_copy(e, k).start()

    def dispatch(e, _):
        want = first + e * slots
        hot = ((cell[0:1] == want) | (cell[1:2] == want)).astype(jnp.float32).astype(z.dtype)

        def part(i, _):
            for j in range(PAIR):
                c = i * PAIR + j
                block = ring[RING - 1, pl.ds(pl.multiple_of(c * tokens, tokens), tokens), :]
                v = jnp.dot(hot, block, preferred_element_type=jnp.float32).astype(z.dtype)
                cols = pl.ds(pl.multiple_of(c * DT, DT), DT)
                z[e, rows(me), cols] = v[:slots]
                sent[e, :, cols] = v[slots:]

            @pl.when((i == 0) & (e > 0))
            def _():
                send(e - 1)

            return 0

        return lax.fori_loop(0, back, part, 0)

    lax.fori_loop(0, experts, dispatch, 0)

    def give_back(e, s):
        for k in (2, 3, 1):
            o_copy(e, s, k).start()
        o_local(e, s).start()

    def given(e):
        def one(s, _):
            for k in (1, 2, 3):
                o_copy(e, s, k).wait_send()
            o_local(e, s).wait()
            return 0

        lax.fori_loop(0, back, one, 0)

    def up(e, s, n):
        g = e * steps + s
        for i in range(n):
            w_issue(g + AHEAD + i)
        for i in range(n):
            at = lax.rem(g + i, RING)
            for j, w in enumerate((wg, wu)):
                pltpu.make_async_copy(
                    w.at[0, :, pl.ds(0, FT)], ring.at[at, pl.ds(0, d), pl.ds(j * FT, FT)], w_sem.at[at, j]
                ).wait()
        for i in range(n):
            both = jnp.dot(z[e], ring[lax.rem(g + i, RING), :d, :], preferred_element_type=jnp.float32)
            a, b = both[:, :FT], both[:, FT:]
            h[:, pl.ds(pl.multiple_of((s + i) * FT, FT), FT)] = (jax.nn.silu(a) * b).astype(h.dtype)

    def down(e, s, n):
        g = e * steps + n1 + s
        for i in range(n):
            w_issue(g + AHEAD + i)
        for i in range(n):
            at = lax.rem(g + i, RING)
            pltpu.make_async_copy(wd.at[0, :, pl.ds(0, DT)], ring.at[at], w_sem.at[at, 0]).wait()

        @pl.when(s > 0)
        def _():
            give_back(e, s // PAIR - 1)

        for i in range(n):
            c = pl.ds(pl.multiple_of((s + i) * DT, DT), DT)
            o[lax.rem(e, 2), :, c] = jnp.dot(
                h[...], ring[lax.rem(g + i, RING)], preferred_element_type=jnp.float32
            ).astype(o.dtype)

    def in_pairs(step, e, n):
        def one(i, _):
            step(e, i * PAIR, PAIR)
            return 0

        lax.fori_loop(0, n // PAIR, one, 0)
        if n % PAIR:
            step(e, n - n % PAIR, n % PAIR)

    def expert(e, _):
        for k in (1, 2, 3):
            z_arrival(e, k).wait_recv()

        @pl.when(e == 0)
        def _():
            send(experts - 1)

        @pl.when(e > 0)
        def _():
            give_back(e - 1, back - 1)

        in_pairs(up, e, n1)

        @pl.when(e >= 2)
        def _():
            given(e - 2)

        in_pairs(down, e, n2)
        return 0

    lax.fori_loop(0, experts, expert, 0)
    given(experts - 2)
    give_back(experts - 1, back - 1)
    given(experts - 1)

    def last(e, _):
        for k in (1, 2, 3):
            z_copy(e, k).wait_send()

        def one(s, _):
            for k in (1, 2, 3):
                o_arrival(e, s, k).wait_recv()
            return 0

        return lax.fori_loop(0, back, one, 0)

    lax.fori_loop(0, experts, last, 0)


def moe(expert, slot, x, wg, wu, wd, members, slots):
    experts, d, f = wg.shape
    back, dma, rows = d // (DT * PAIR), pltpu.SemaphoreType.DMA, members * slots
    vmem, anywhere = pl.BlockSpec(memory_space=pltpu.VMEM), pl.BlockSpec(memory_space=pl.ANY)
    return pl.pallas_call(
        ffn_kernel,
        out_shape=jax.ShapeDtypeStruct((members, experts, slots, d), x.dtype),
        in_specs=[vmem, vmem] + [anywhere] * 4,
        out_specs=anywhere,
        scratch_shapes=[
            pltpu.VMEM((experts, rows - slots, d), x.dtype),
            pltpu.VMEM((experts, rows, d), x.dtype),
            pltpu.VMEM((rows, f), x.dtype),
            pltpu.VMEM((2, rows, d), x.dtype),
            pltpu.VMEM((RING, f, 2 * FT), x.dtype),
            dma((d // DT,)),
            dma((RING, 2)),
            dma((experts, 3)),
            dma((experts, 3)),
            dma((experts, back, 3)),
            dma((experts, back, 3)),
            dma((experts, back)),
        ],
        compiler_params=pltpu.CompilerParams(
            collective_id=0, has_side_effects=True, vmem_limit_bytes=67_000_000
        ),
    )(expert, slot, x, wg, wu, wd)


def combine_kernel(expert_ref, slot_ref, gate_ref, r_ref, y_ref, weights, *, slots):
    @pl.when(pl.program_id(0) == 0)
    def _():
        cell, gate = cell_of(expert_ref, slot_ref, slots), gate_ref[...].astype(jnp.bfloat16).astype(jnp.float32)
        q = lax.broadcasted_iota(jnp.int32, (r_ref.shape[0], cell.shape[1]), 0)
        w = sum(jnp.where(cell[j : j + 1] == q, gate[j : j + 1], 0.0) for j in range(cell.shape[0]))
        weights[...] = w.T.astype(jnp.bfloat16)

    y_ref[...] = jnp.dot(weights[...], r_ref[...], preferred_element_type=jnp.float32).astype(y_ref.dtype)


def combine(expert, slot, gate, r, slots):
    (top, tokens), (cells, d), width = expert.shape, r.shape, 512
    small = pl.BlockSpec((top, tokens), lambda i: (0, 0))
    return pl.pallas_call(
        functools.partial(combine_kernel, slots=slots),
        out_shape=jax.ShapeDtypeStruct((tokens, d), jnp.bfloat16),
        grid=(d // width,),
        in_specs=[small, small, small, pl.BlockSpec((cells, width), lambda i: (0, i))],
        out_specs=pl.BlockSpec((tokens, width), lambda i: (0, i)),
        scratch_shapes=[pltpu.VMEM((tokens, cells), jnp.bfloat16)],
    )(expert, slot, gate, r)


def solution(mesh):
    members = mesh.shape["ep"]

    def step(x, expert, slot, gate, w_gate, w_up, w_down):
        x, expert, slot, gate = x[0, 0], expert[0, 0].T, slot[0, 0].T, gate[0, 0].T
        (top, tokens), experts = expert.shape, members * w_gate.shape[0]
        slots = 5 * tokens * top // (4 * experts)
        r = moe(expert, slot, x, w_gate, w_up, w_down, members, slots)
        return combine(expert, slot, gate, r.reshape(experts * slots, x.shape[1]), slots)[None, None]

    own, weights = P("dp", "ep"), P("ep")
    return jax.shard_map(
        step, mesh=mesh, in_specs=(own, own, own, own, weights, weights, weights), out_specs=own, check_vma=False
    )
```

time: 315 us -> 286 us (0.908)
  matrix products: 30.3 us -> 0 us
  Pallas kernels: 279 us -> 286 us
  local copies, waits for them, and re-layouts: 5.74 us -> 0 us
    dot_general x4 -> x0, matrix products: 30.3 us -> none  [einsum(): return jnp.einsum(form, a.astype(jnp.float32), b.astype(jnp.float32))]
    pallas_call x1 -> x2, Pallas kernels: 279 us -> 286 us  [the longest x1 274 us: moe(): pl.pallas_call(ffn_kernel, out_shape=jax.ShapeDtypeStruct((members, exper...]
    dot_general x2 -> x0, local copies, waits for them, and re-layouts: 3.18 us -> none  [einsum(): return jnp.einsum(form, a.astype(jnp.float32), b.astype(jnp.float32))]
where the time goes in v2:
time: 286 us
  Pallas kernels  286 us (100%)
    pallas_call x1, Pallas kernels, moe(): pl.pallas_call(ffn_kernel, out_shape=jax.ShapeDtypeStruct((members, exper...  274 us
    pallas_call x1, Pallas kernels, combine(): pl.pallas_call(functools.partial(combine_kernel, slots=slots), out_shape=...  11.9 us

profile of v2, /device:TPU:0, one launch (start us, length us, event | category | flops | bytes accessed | tf_op | source)
XLA Modules:
  0.0 286.1 jit_solution(8997024861007156172)
XLA Ops:
  0.0 274.2 %shard_map.73 = bf16[4,4,80,4096]{3,2,1,0:T(8,128)(2,1)} custom-call(s32[2,512]{1,0:T(2,128)} %bitcast.14, s32[2,512]{1,0:T(2,128)} %bitcast.16, bf16[512,4096]{1,0:T(8,128)(2,1)} %bitcast.13, bf16[4,4096,6400]{2,1,0:T(8,128)(2,1)} %wg.1, bf16[4,4096,6400]{2,1,0:T(8,128)(2,1)} %wu.1, bf16[4,6400,4096]{2,1,0:T(8,128)(2,1)} %wd.1), custom_call_target="tpu_custom_call" | custom-call | tf_op jit(solution)/shard_map/pallas_call | solution.py:235
  274.2 11.9 %shard_map.74 = bf16[512,4096]{1,0:T(8,128)(2,1)} custom-call(s32[2,512]{1,0:T(2,128)} %bitcast.15, s32[2,512]{1,0:T(2,128)} %bitcast.17, f32[2,512]{1,0:T(2,128)} %bitcast.18, bf16[1280,4096]{1,0:T(8,128)(2,1)} %bitcast.12), custom_call_target="tpu_custom_call" | custom-call | tf_op jit(solution)/shard_map/pallas_call | solution.py:274

commit v3 on v2

--- a/solution.py
+++ b/solution.py
@@ -10,6 +10,7 @@
 MESH = pl.DeviceIdType.MESH
 FT, DT, RING, PAIR = 256, 512, 5, 2
 AHEAD = RING - PAIR
+CHUNKS, GROUP = 4, 4
 
 
 def cell_of(expert_ref, slot_ref, slots):
@@ -18,8 +19,8 @@
 
 
 def ffn_kernel(
-    expert_ref, slot_ref, x_ref, wg, wu, wd, r_ref, sent, z, h, o, ring,
-    x_sem, w_sem, z_send, z_recv, o_send, o_recv, o_own,
+    expert_ref, slot_ref, x_ref, wg, wu, wd, r_ref, sent, z, h, acc, ring,
+    x_sem, w_sem, z_send, z_recv, c_send, c_recv, o_send, o_recv, o_own,
 ):
     experts, rows_z, d = z.shape
     members = r_ref.shape[0]
@@ -28,6 +29,8 @@
     n1, n2 = f // FT, d // DT
     steps, total, back = n1 + n2, experts * (n1 + n2), n2 // PAIR
     me, group = lax.axis_index("ep"), lax.axis_index("dp")
+    depth, early = d // CHUNKS, acc.shape[0]
+    starts = CHUNKS * early // GROUP
 
     def peer(k):
         return me ^ k
@@ -43,7 +46,19 @@
     def w_issue(g):
         e, s, at = g // steps, lax.rem(g, steps), lax.rem(g, RING)
 
-        @pl.when((s < n1) & (g < total))
+        @pl.when(g < starts)
+        def _():
+            q, m = g // (early // GROUP), lax.rem(g, early // GROUP)
+            for i in range(GROUP):
+                c = pl.ds(pl.multiple_of((m * GROUP + i) * FT, FT), FT)
+                for j, w in enumerate((wg, wu)):
+                    pltpu.make_async_copy(
+                        w.at[0, pl.ds(pl.multiple_of(q * depth, depth), depth), c],
+                        ring.at[at, pl.ds(i * depth, depth), pl.ds(j * FT, FT)],
+                        w_sem.at[at, j],
+                    ).start()
+
+        @pl.when((s < n1) & (g < total) & (g >= starts))
         def _():
             c = pl.ds(pl.multiple_of(s * FT, FT), FT)
             for j, w in enumerate((wg, wu)):
@@ -62,6 +77,20 @@
             device_id=(group, peer(k)), device_id_type=MESH,
         )
 
+    def chunk_copy(q, k):
+        c = pl.ds(pl.multiple_of(q * depth, depth), depth)
+        return pltpu.make_async_remote_copy(
+            sent.at[0, pl.ds((k - 1) * slots, slots), c], z.at[0, rows(me), c], c_send.at[q, k - 1],
+            c_recv.at[q, k - 1], device_id=(group, peer(k)), device_id_type=MESH,
+        )
+
+    def chunk_arrival(q, k):
+        c = pl.ds(pl.multiple_of(q * depth, depth), depth)
+        return pltpu.make_async_remote_copy(
+            sent.at[0, pl.ds((k - 1) * slots, slots), c], z.at[0, rows(peer(k)), c], c_send.at[q, k - 1],
+            c_recv.at[q, k - 1], device_id=(group, peer(k)), device_id_type=MESH,
+        )
+
     def z_arrival(e, k):
         return pltpu.make_async_remote_copy(
             sent.at[e, pl.ds((k - 1) * slots, slots)], z.at[e, rows(peer(k))], z_send.at[e, k - 1],
@@ -74,20 +103,20 @@
     def o_copy(e, s, k):
         c = back_columns(s)
         return pltpu.make_async_remote_copy(
-            o.at[lax.rem(e, 2), rows(peer(k)), c], r_ref.at[me, e, :, c], o_send.at[e, s, k - 1],
+            z.at[e, rows(peer(k)), c], r_ref.at[me, e, :, c], o_send.at[e, s, k - 1],
             o_recv.at[e, s, k - 1], device_id=(group, peer(k)), device_id_type=MESH,
         )
 
     def o_arrival(e, s, k):
         c = back_columns(s)
         return pltpu.make_async_remote_copy(
-            o.at[lax.rem(e, 2), rows(me), c], r_ref.at[peer(k), e, :, c], o_send.at[e, s, k - 1],
+            z.at[e, rows(me), c], r_ref.at[peer(k), e, :, c], o_send.at[e, s, k - 1],
             o_recv.at[e, s, k - 1], device_id=(group, peer(k)), device_id_type=MESH,
         )
 
     def o_local(e, s):
         c = back_columns(s)
-        return pltpu.make_async_copy(o.at[lax.rem(e, 2), rows(me), c], r_ref.at[me, e, :, c], o_own.at[e, s])
+        return pltpu.make_async_copy(z.at[e, rows(me), c], r_ref.at[me, e, :, c], o_own.at[e, s])
 
     for j in range(n2):
         x_copy(j).start()
@@ -98,7 +127,7 @@
         w_issue(jnp.int32(g))
 
     cell = cell_of(expert_ref, slot_ref, slots)
-    row = lax.broadcasted_iota(jnp.int32, (rows_z, tokens), 0)
+    row = lax.broadcasted_iota(jnp.int32, (rows_z, 1), 0)
     k_of = sum((row >= i * slots).astype(jnp.int32) for i in range(1, members))
     first = (me ^ k_of) * (experts * slots) + row - k_of * slots
     for j in range(n2):
@@ -108,6 +137,10 @@
     def send(e):
         for k in (2, 3, 1):
             z_copy(e, k).start()
+
+    def send_chunk(q):
+        for k in (2, 3, 1):
+            chunk_copy(q, k).start()
 
     def dispatch(e, _):
         want = first + e * slots
@@ -122,7 +155,15 @@
                 z[e, rows(me), cols] = v[:slots]
                 sent[e, :, cols] = v[slots:]
 
-            @pl.when((i == 0) & (e > 0))
+            @pl.when((e == 0) & (i > 0))
+            def _():
+                send_chunk(i - 1)
+
+            @pl.when((e == 1) & (i == 0))
+            def _():
+                send_chunk(back - 1)
+
+            @pl.when((e > 1) & (i == 0))
             def _():
                 send(e - 1)
 
@@ -146,16 +187,41 @@
 
         lax.fori_loop(0, back, one, 0)
 
+    def up_wait(at):
+        for j, w in enumerate((wg, wu)):
+            pltpu.make_async_copy(
+                w.at[0, :, pl.ds(0, FT)], ring.at[at, pl.ds(0, d), pl.ds(j * FT, FT)], w_sem.at[at, j]
+            ).wait()
+
+    def start_step(final, g, _):
+        q, m = g // (early // GROUP), lax.rem(g, early // GROUP)
+
+        @pl.when(m == 0)
+        def _():
+            for k in (1, 2, 3):
+                chunk_arrival(q, k).wait_recv()
+
+        at = lax.rem(g, RING)
+        w_issue(g + AHEAD)
+        up_wait(at)
+        c = pl.ds(pl.multiple_of(q * depth, depth), depth)
+        for i in range(GROUP):
+            t = m * GROUP + i
+            w = ring[at, i * depth : (i + 1) * depth, :]
+            both = acc[t] + jnp.dot(z[0, :, c], w, preferred_element_type=jnp.float32)
+            if final:
+                a, b = both[:, :FT], both[:, FT:]
+                h[:, pl.ds(pl.multiple_of(t * FT, FT), FT)] = (jax.nn.silu(a) * b).astype(h.dtype)
+            else:
+                acc[t] = both
+        return 0
+
     def up(e, s, n):
         g = e * steps + s
         for i in range(n):
             w_issue(g + AHEAD + i)
         for i in range(n):
-            at = lax.rem(g + i, RING)
-            for j, w in enumerate((wg, wu)):
-                pltpu.make_async_copy(
-                    w.at[0, :, pl.ds(0, FT)], ring.at[at, pl.ds(0, d), pl.ds(j * FT, FT)], w_sem.at[at, j]
-                ).wait()
+            up_wait(lax.rem(g + i, RING))
         for i in range(n):
             both = jnp.dot(z[e], ring[lax.rem(g + i, RING), :d, :], preferred_element_type=jnp.float32)
             a, b = both[:, :FT], both[:, FT:]
@@ -175,48 +241,52 @@
 
         for i in range(n):
             c = pl.ds(pl.multiple_of((s + i) * DT, DT), DT)
-            o[lax.rem(e, 2), :, c] = jnp.dot(
+            z[e, :, c] = jnp.dot(
                 h[...], ring[lax.rem(g + i, RING)], preferred_element_type=jnp.float32
-            ).astype(o.dtype)
-
-    def in_pairs(step, e, n):
+            ).astype(z.dtype)
+
+    def in_pairs(step, e, done, n):
         def one(i, _):
             step(e, i * PAIR, PAIR)
             return 0
 
-        lax.fori_loop(0, n // PAIR, one, 0)
+        lax.fori_loop(done // PAIR, n // PAIR, one, 0)
         if n % PAIR:
             step(e, n - n % PAIR, n % PAIR)
 
     def expert(e, _):
-        for k in (1, 2, 3):
-            z_arrival(e, k).wait_recv()
-
-        @pl.when(e == 0)
-        def _():
-            send(experts - 1)
-
         @pl.when(e > 0)
         def _():
+            for k in (1, 2, 3):
+                z_arrival(e, k).wait_recv()
             give_back(e - 1, back - 1)
 
-        in_pairs(up, e, n1)
-
-        @pl.when(e >= 2)
-        def _():
-            given(e - 2)
-
-        in_pairs(down, e, n2)
+        in_pairs(up, e, early * (1 - (e + experts - 1) // experts), n1)
+        in_pairs(down, e, 0, n2)
         return 0
 
+    def clear(t, _):
+        acc[t] = jnp.zeros(acc.shape[1:], acc.dtype)
+        return 0
+
+    lax.fori_loop(0, early, clear, 0)
+    send(experts - 1)
+    lax.fori_loop(0, starts - early // GROUP, functools.partial(start_step, False), 0)
+    lax.fori_loop(starts - early // GROUP, starts, functools.partial(start_step, True), 0)
     lax.fori_loop(0, experts, expert, 0)
-    given(experts - 2)
+    for e in range(experts - 1):
+        given(e)
     give_back(experts - 1, back - 1)
     given(experts - 1)
+    for q in range(CHUNKS):
+        for k in (1, 2, 3):
+            chunk_copy(q, k).wait_send()
 
     def last(e, _):
-        for k in (1, 2, 3):
-            z_copy(e, k).wait_send()
+        @pl.when(e > 0)
+        def _():
+            for k in (1, 2, 3):
+                z_copy(e, k).wait_send()
 
         def one(s, _):
             for k in (1, 2, 3):
@@ -231,6 +301,7 @@
 def moe(expert, slot, x, wg, wu, wd, members, slots):
     experts, d, f = wg.shape
     back, dma, rows = d // (DT * PAIR), pltpu.SemaphoreType.DMA, members * slots
+    n_early = GROUP * 3
     vmem, anywhere = pl.BlockSpec(memory_space=pltpu.VMEM), pl.BlockSpec(memory_space=pl.ANY)
     return pl.pallas_call(
         ffn_kernel,
@@ -241,12 +312,14 @@
             pltpu.VMEM((experts, rows - slots, d), x.dtype),
             pltpu.VMEM((experts, rows, d), x.dtype),
             pltpu.VMEM((rows, f), x.dtype),
-            pltpu.VMEM((2, rows, d), x.dtype),
+            pltpu.VMEM((n_early, rows, 2 * FT), jnp.float32),
             pltpu.VMEM((RING, f, 2 * FT), x.dtype),
             dma((d // DT,)),
             dma((RING, 2)),
             dma((experts, 3)),
             dma((experts, 3)),
+            dma((CHUNKS, 3)),
+            dma((CHUNKS, 3)),
             dma((experts, back, 3)),
             dma((experts, back, 3)),
             dma((experts, back)),
@@ -261,9 +334,11 @@
     @pl.when(pl.program_id(0) == 0)
     def _():
         cell, gate = cell_of(expert_ref, slot_ref, slots), gate_ref[...].astype(jnp.bfloat16).astype(jnp.float32)
-        q = lax.broadcasted_iota(jnp.int32, (r_ref.shape[0], cell.shape[1]), 0)
-        w = sum(jnp.where(cell[j : j + 1] == q, gate[j : j + 1], 0.0) for j in range(cell.shape[0]))
-        weights[...] = w.T.astype(jnp.bfloat16)
+        top = cell.shape[0]
+        both = jnp.concatenate([cell.astype(jnp.float32), gate] * (4 // top), axis=0).T
+        q = lax.broadcasted_iota(jnp.int32, weights.shape, 1).astype(jnp.float32)
+        w = sum(jnp.where(both[:, j : j + 1] == q, both[:, top + j : top + j + 1], 0.0) for j in range(top))
+        weights[...] = w.astype(jnp.bfloat16)
 
     y_ref[...] = jnp.dot(weights[...], r_ref[...], preferred_element_type=jnp.float32).astype(y_ref.dtype)
 

time: 286 us -> 275 us (0.962)
  Pallas kernels: 286 us -> 274 us
    pallas_call x1, Pallas kernels: 274 us -> 262 us  [moe(): pl.pallas_call(ffn_kernel, out_shape=jax.ShapeDtypeStruct((members, exper...]
where the time goes in v3:
time: 275 us; the launch traced here: 274 us
  Pallas kernels  274 us (100%)
    pallas_call x1, Pallas kernels, moe(): pl.pallas_call(ffn_kernel, out_shape=jax.ShapeDtypeStruct((members, exper...  262 us
    pallas_call x1, Pallas kernels, combine(): pl.pallas_call(functools.partial(combine_kernel, slots=slots), out_shape=...  12.1 us

profile of v3, /device:TPU:0, one launch (start us, length us, event | category | flops | bytes accessed | tf_op | source)
XLA Modules:
  0.0 274.3 jit_solution(14008395154031411260)
XLA Ops:
  0.0 262.2 %shard_map.73 = bf16[4,4,80,4096]{3,2,1,0:T(8,128)(2,1)} custom-call(s32[2,512]{1,0:T(2,128)} %bitcast.14, s32[2,512]{1,0:T(2,128)} %bitcast.16, bf16[512,4096]{1,0:T(8,128)(2,1)} %bitcast.13, bf16[4,4096,6400]{2,1,0:T(8,128)(2,1)} %wg.1, bf16[4,4096,6400]{2,1,0:T(8,128)(2,1)} %wu.1, bf16[4,6400,4096]{2,1,0:T(8,128)(2,1)} %wd.1), custom_call_target="tpu_custom_call" | custom-call | tf_op jit(solution)/shard_map/pallas_call | solution.py:306
  262.2 12.1 %shard_map.74 = bf16[512,4096]{1,0:T(8,128)(2,1)} custom-call(s32[2,512]{1,0:T(2,128)} %bitcast.15, s32[2,512]{1,0:T(2,128)} %bitcast.17, f32[2,512]{1,0:T(2,128)} %bitcast.18, bf16[1280,4096]{1,0:T(8,128)(2,1)} %bitcast.12), custom_call_target="tpu_custom_call" | custom-call | tf_op jit(solution)/shard_map/pallas_call | solution.py:349

commit v4 on v3

--- a/solution.py
+++ b/solution.py
@@ -19,8 +19,8 @@
 
 
 def ffn_kernel(
-    expert_ref, slot_ref, x_ref, wg, wu, wd, r_ref, sent, z, h, acc, ring,
-    x_sem, w_sem, z_send, z_recv, c_send, c_recv, o_send, o_recv, o_own,
+    expert_ref, slot_ref, gate_ref, x_ref, wg, wu, wd, y_ref, r_ref, sent, z, h, acc, ring, weights,
+    x_sem, w_sem, z_send, z_recv, c_send, c_recv, o_send, o_recv, o_own, r_sem, y_sem,
 ):
     experts, rows_z, d = z.shape
     members = r_ref.shape[0]
@@ -103,20 +103,20 @@
     def o_copy(e, s, k):
         c = back_columns(s)
         return pltpu.make_async_remote_copy(
-            z.at[e, rows(peer(k)), c], r_ref.at[me, e, :, c], o_send.at[e, s, k - 1],
+            z.at[e, rows(peer(k)), c], r_ref.at[me, rows(e), c], o_send.at[e, s, k - 1],
             o_recv.at[e, s, k - 1], device_id=(group, peer(k)), device_id_type=MESH,
         )
 
     def o_arrival(e, s, k):
         c = back_columns(s)
         return pltpu.make_async_remote_copy(
-            z.at[e, rows(me), c], r_ref.at[peer(k), e, :, c], o_send.at[e, s, k - 1],
+            z.at[e, rows(me), c], r_ref.at[peer(k), rows(e), c], o_send.at[e, s, k - 1],
             o_recv.at[e, s, k - 1], device_id=(group, peer(k)), device_id_type=MESH,
         )
 
     def o_local(e, s):
         c = back_columns(s)
-        return pltpu.make_async_copy(z.at[e, rows(me), c], r_ref.at[me, e, :, c], o_own.at[e, s])
+        return pltpu.make_async_copy(z.at[e, rows(me), c], r_ref.at[me, rows(e), c], o_own.at[e, s])
 
     for j in range(n2):
         x_copy(j).start()
@@ -177,15 +177,6 @@
         for k in (2, 3, 1):
             o_copy(e, s, k).start()
         o_local(e, s).start()
-
-    def given(e):
-        def one(s, _):
-            for k in (1, 2, 3):
-                o_copy(e, s, k).wait_send()
-            o_local(e, s).wait()
-            return 0
-
-        lax.fori_loop(0, back, one, 0)
 
     def up_wait(at):
         for j, w in enumerate((wg, wu)):
@@ -271,13 +262,66 @@
 
     lax.fori_loop(0, early, clear, 0)
     send(experts - 1)
+    top = cell.shape[0]
+    gate = gate_ref[...].astype(jnp.bfloat16).astype(jnp.float32)
+    both = jnp.concatenate([cell.astype(jnp.float32), gate] * (4 // top), axis=0).T
+
+    def weigh(i, _):
+        c = pl.ds(pl.multiple_of(i * 256, 256), 256)
+        q = (lax.broadcasted_iota(jnp.int32, (tokens, 256), 1) + i * 256).astype(jnp.float32)
+        w = sum(jnp.where(both[:, j : j + 1] == q, both[:, top + j : top + j + 1], 0.0) for j in range(top))
+        weights[:, c] = w.astype(weights.dtype)
+        return 0
+
+    lax.fori_loop(0, weights.shape[1] // 256, weigh, 0)
     lax.fori_loop(0, starts - early // GROUP, functools.partial(start_step, False), 0)
     lax.fori_loop(starts - early // GROUP, starts, functools.partial(start_step, True), 0)
     lax.fori_loop(0, experts, expert, 0)
-    for e in range(experts - 1):
-        given(e)
     give_back(experts - 1, back - 1)
-    given(experts - 1)
+
+    cells, per = members * rows_z, f // (members * rows_z)
+
+    def r_copy(c, i):
+        return pltpu.make_async_copy(
+            r_ref.at[i, :, pl.ds(pl.multiple_of(c * DT, DT), DT)],
+            ring.at[c // per, pl.ds(pl.multiple_of(lax.rem(c, per) * cells + i * rows_z, rows_z), rows_z)],
+            r_sem.at[c, i],
+        )
+
+    def y_copy(c):
+        return pltpu.make_async_copy(
+            ring.at[2, pl.ds(pl.multiple_of(c * tokens, tokens), tokens)],
+            y_ref.at[:, pl.ds(pl.multiple_of(c * DT, DT), DT)],
+            y_sem.at[c],
+        )
+
+    def arrived(s):
+        def one(e, _):
+            for k in (1, 2, 3):
+                o_arrival(e, s, k).wait_recv()
+            o_local(e, s).wait()
+            return 0
+
+        lax.fori_loop(0, experts, one, 0)
+
+    def merge(s, _):
+        arrived(s)
+        for j in range(PAIR):
+            for i in range(members):
+                r_copy(s * PAIR + j, i).start()
+        for j in range(PAIR):
+            for i in range(members):
+                r_copy(s * PAIR + j, i).wait()
+        for j in range(PAIR):
+            c = s * PAIR + j
+            block = ring[c // per, pl.ds(pl.multiple_of(lax.rem(c, per) * cells, cells), cells), :]
+            v = jnp.dot(weights[...], block, preferred_element_type=jnp.float32)
+            ring[2, pl.ds(pl.multiple_of(c * tokens, tokens), tokens), :] = v.astype(ring.dtype)
+        for j in range(PAIR):
+            y_copy(s * PAIR + j).start()
+        return 0
+
+    lax.fori_loop(0, back, merge, 0)
     for q in range(CHUNKS):
         for k in (1, 2, 3):
             chunk_copy(q, k).wait_send()
@@ -290,30 +334,40 @@
 
         def one(s, _):
             for k in (1, 2, 3):
-                o_arrival(e, s, k).wait_recv()
+                o_copy(e, s, k).wait_send()
             return 0
 
         return lax.fori_loop(0, back, one, 0)
 
     lax.fori_loop(0, experts, last, 0)
 
-
-def moe(expert, slot, x, wg, wu, wd, members, slots):
+    def written(c, _):
+        y_copy(c).wait()
+        return 0
+
+    lax.fori_loop(0, n2, written, 0)
+
+
+def moe(expert, slot, gate, x, wg, wu, wd, members, slots):
     experts, d, f = wg.shape
     back, dma, rows = d // (DT * PAIR), pltpu.SemaphoreType.DMA, members * slots
     n_early = GROUP * 3
     vmem, anywhere = pl.BlockSpec(memory_space=pltpu.VMEM), pl.BlockSpec(memory_space=pl.ANY)
     return pl.pallas_call(
         ffn_kernel,
-        out_shape=jax.ShapeDtypeStruct((members, experts, slots, d), x.dtype),
-        in_specs=[vmem, vmem] + [anywhere] * 4,
-        out_specs=anywhere,
+        out_shape=(
+            jax.ShapeDtypeStruct(x.shape, x.dtype),
+            jax.ShapeDtypeStruct((members, rows, d), x.dtype),
+        ),
+        in_specs=[vmem] * 3 + [anywhere] * 4,
+        out_specs=(anywhere, anywhere),
         scratch_shapes=[
             pltpu.VMEM((experts, rows - slots, d), x.dtype),
             pltpu.VMEM((experts, rows, d), x.dtype),
             pltpu.VMEM((rows, f), x.dtype),
             pltpu.VMEM((n_early, rows, 2 * FT), jnp.float32),
             pltpu.VMEM((RING, f, 2 * FT), x.dtype),
+            pltpu.VMEM((x.shape[0], members * rows), x.dtype),
             dma((d // DT,)),
             dma((RING, 2)),
             dma((experts, 3)),
@@ -323,37 +377,13 @@
             dma((experts, back, 3)),
             dma((experts, back, 3)),
             dma((experts, back)),
+            dma((d // DT, members)),
+            dma((d // DT,)),
         ],
         compiler_params=pltpu.CompilerParams(
             collective_id=0, has_side_effects=True, vmem_limit_bytes=67_000_000
         ),
-    )(expert, slot, x, wg, wu, wd)
-
-
-def combine_kernel(expert_ref, slot_ref, gate_ref, r_ref, y_ref, weights, *, slots):
-    @pl.when(pl.program_id(0) == 0)
-    def _():
-        cell, gate = cell_of(expert_ref, slot_ref, slots), gate_ref[...].astype(jnp.bfloat16).astype(jnp.float32)
-        top = cell.shape[0]
-        both = jnp.concatenate([cell.astype(jnp.float32), gate] * (4 // top), axis=0).T
-        q = lax.broadcasted_iota(jnp.int32, weights.shape, 1).astype(jnp.float32)
-        w = sum(jnp.where(both[:, j : j + 1] == q, both[:, top + j : top + j + 1], 0.0) for j in range(top))
-        weights[...] = w.astype(jnp.bfloat16)
-
-    y_ref[...] = jnp.dot(weights[...], r_ref[...], preferred_element_type=jnp.float32).astype(y_ref.dtype)
-
-
-def combine(expert, slot, gate, r, slots):
-    (top, tokens), (cells, d), width = expert.shape, r.shape, 512
-    small = pl.BlockSpec((top, tokens), lambda i: (0, 0))
-    return pl.pallas_call(
-        functools.partial(combine_kernel, slots=slots),
-        out_shape=jax.ShapeDtypeStruct((tokens, d), jnp.bfloat16),
-        grid=(d // width,),
-        in_specs=[small, small, small, pl.BlockSpec((cells, width), lambda i: (0, i))],
-        out_specs=pl.BlockSpec((tokens, width), lambda i: (0, i)),
-        scratch_shapes=[pltpu.VMEM((tokens, cells), jnp.bfloat16)],
-    )(expert, slot, gate, r)
+    )(expert, slot, gate, x, wg, wu, wd)[0]
 
 
 def solution(mesh):
@@ -363,8 +393,7 @@
         x, expert, slot, gate = x[0, 0], expert[0, 0].T, slot[0, 0].T, gate[0, 0].T
         (top, tokens), experts = expert.shape, members * w_gate.shape[0]
         slots = 5 * tokens * top // (4 * experts)
-        r = moe(expert, slot, x, w_gate, w_up, w_down, members, slots)
-        return combine(expert, slot, gate, r.reshape(experts * slots, x.shape[1]), slots)[None, None]
+        return moe(expert, slot, gate, x, w_gate, w_up, w_down, members, slots)[None, None]
 
     own, weights = P("dp", "ep"), P("ep")
     return jax.shard_map(

time: 275 us -> 272 us (0.989)
  Pallas kernels: 274 us -> 267 us
  local copies, waits for them, and re-layouts: 0 us -> 4.7 us
    pallas_call x2 -> x1, Pallas kernels: 274 us -> 267 us  [moe(): pl.pallas_call(ffn_kernel, out_shape=(jax.ShapeDtypeStruct(x.shape, x.dty...]
    unnamed x0 -> x1, local copies, waits for them, and re-layouts: none -> 4.7 us
where the time goes in v4:
time: 272 us
  Pallas kernels  267 us (98%)
  local copies, waits for them, and re-layouts  4.7 us (2%)
    pallas_call x1, Pallas kernels, moe(): pl.pallas_call(ffn_kernel, out_shape=(jax.ShapeDtypeStruct(x.shape, x.dty...  267 us

profile of v4, /device:TPU:0, one launch (start us, length us, event | category | flops | bytes accessed | tf_op | source)
XLA Modules:
  0.0 271.6 jit_solution(17580519265672263678)
XLA Ops:
  0.0 266.9 %shard_map.73 = (bf16[512,4096]{1,0:T(8,128)(2,1)}, bf16[4,320,4096]{2,1,0:T(8,128)(2,1)}) custom-call(s32[2,512]{1,0:T(2,128)} %bitcast.13, s32[2,512]{1,0:T(2,128)} %bitcast.14, f32[2,512]{1,0:T(2,128)} %bitcast.15, bf16[512,4096]{1,0:T(8,128)(2,1)} %bitcast.11, bf16[4,4096,6400]{2,1,0:T(8,128)(2,1)} %wg.1, bf16[4,4096,6400]{2,1,0:T(8,128)(2,1)} %wu.1, ...), custom_call_target="tpu_custom_call" | custom-call | tf_op jit(solution)/shard_map/pallas_call | solution.py:356
  266.9 4.7 %copy.9 = bf16[1,1,512,4096]{3,2,1,0:T(8,128)(2,1)} copy(bf16[1,1,512,4096]{3,2,1,0:T(8,128)(2,1)} %bitcast.12) | data formatting | bytes 8388608

commit v5 on v4

--- a/solution.py
+++ b/solution.py
@@ -19,8 +19,8 @@
 
 
 def ffn_kernel(
-    expert_ref, slot_ref, gate_ref, x_ref, wg, wu, wd, y_ref, r_ref, sent, z, h, acc, ring, weights,
-    x_sem, w_sem, z_send, z_recv, c_send, c_recv, o_send, o_recv, o_own, r_sem, y_sem,
+    expert_ref, slot_ref, gate_ref, x_ref, wg, wu, wd, y_ref, r_ref, sent, z, h, acc, ring,
+    x_sem, w_sem, z_send, z_recv, c_send, c_recv, o_send, o_recv, o_own, r_sem, y_sem, free,
 ):
     experts, rows_z, d = z.shape
     members = r_ref.shape[0]
@@ -40,7 +40,9 @@
 
     def x_copy(j):
         return pltpu.make_async_copy(
-            x_ref.at[:, pl.ds(j * DT, DT)], ring.at[RING - 1, pl.ds(j * tokens, tokens)], x_sem.at[j]
+            x_ref.at[:, pl.ds(pl.multiple_of(j * DT, DT), DT)],
+            ring.at[RING - 1, pl.ds(pl.multiple_of(j * tokens, tokens), tokens)],
+            x_sem.at[j],
         )
 
     def w_issue(g):
@@ -73,27 +75,27 @@
 
     def z_copy(e, k):
         return pltpu.make_async_remote_copy(
-            sent.at[e, pl.ds((k - 1) * slots, slots)], z.at[e, rows(me)], z_send.at[e, k - 1], z_recv.at[e, k - 1],
+            sent.at[e - 1, pl.ds((k - 1) * slots, slots)], z.at[e, rows(me)], z_send.at[e, k - 1], z_recv.at[e, k - 1],
             device_id=(group, peer(k)), device_id_type=MESH,
         )
 
     def chunk_copy(q, k):
         c = pl.ds(pl.multiple_of(q * depth, depth), depth)
         return pltpu.make_async_remote_copy(
-            sent.at[0, pl.ds((k - 1) * slots, slots), c], z.at[0, rows(me), c], c_send.at[q, k - 1],
+            z.at[experts - 1, rows(peer(k)), c], z.at[0, rows(me), c], c_send.at[q, k - 1],
             c_recv.at[q, k - 1], device_id=(group, peer(k)), device_id_type=MESH,
         )
 
     def chunk_arrival(q, k):
         c = pl.ds(pl.multiple_of(q * depth, depth), depth)
         return pltpu.make_async_remote_copy(
-            sent.at[0, pl.ds((k - 1) * slots, slots), c], z.at[0, rows(peer(k)), c], c_send.at[q, k - 1],
+            z.at[experts - 1, rows(peer(k)), c], z.at[0, rows(peer(k)), c], c_send.at[q, k - 1],
             c_recv.at[q, k - 1], device_id=(group, peer(k)), device_id_type=MESH,
         )
 
     def z_arrival(e, k):
         return pltpu.make_async_remote_copy(
-            sent.at[e, pl.ds((k - 1) * slots, slots)], z.at[e, rows(peer(k))], z_send.at[e, k - 1],
+            sent.at[e - 1, pl.ds((k - 1) * slots, slots)], z.at[e, rows(peer(k))], z_send.at[e, k - 1],
             z_recv.at[e, k - 1], device_id=(group, peer(k)), device_id_type=MESH,
         )
 
@@ -123,15 +125,11 @@
     barrier = pltpu.get_barrier_semaphore()
     for k in (1, 2, 3):
         pl.semaphore_signal(barrier, inc=1, device_id=(group, peer(k)), device_id_type=MESH)
-    for g in range(AHEAD):
-        w_issue(jnp.int32(g))
 
     cell = cell_of(expert_ref, slot_ref, slots)
     row = lax.broadcasted_iota(jnp.int32, (rows_z, 1), 0)
     k_of = sum((row >= i * slots).astype(jnp.int32) for i in range(1, members))
     first = (me ^ k_of) * (experts * slots) + row - k_of * slots
-    for j in range(n2):
-        x_copy(j).wait()
     pl.semaphore_wait(barrier, 3)
 
     def send(e):
@@ -147,13 +145,31 @@
         hot = ((cell[0:1] == want) | (cell[1:2] == want)).astype(jnp.float32).astype(z.dtype)
 
         def part(i, _):
+            @pl.when(e == 0)
+            def _():
+                for j in range(PAIR):
+                    x_copy(i * PAIR + j).wait()
+
+            @pl.when((e == 0) & (i == back - 1))
+            def _():
+                for g in range(AHEAD):
+                    w_issue(jnp.int32(g))
+
             for j in range(PAIR):
                 c = i * PAIR + j
                 block = ring[RING - 1, pl.ds(pl.multiple_of(c * tokens, tokens), tokens), :]
                 v = jnp.dot(hot, block, preferred_element_type=jnp.float32).astype(z.dtype)
                 cols = pl.ds(pl.multiple_of(c * DT, DT), DT)
                 z[e, rows(me), cols] = v[:slots]
-                sent[e, :, cols] = v[slots:]
+
+                @pl.when(e == 0)
+                def _():
+                    for k in (1, 2, 3):
+                        z[experts - 1, rows(peer(k)), cols] = v[k * slots : (k + 1) * slots]
+
+                @pl.when(e > 0)
+                def _():
+                    sent[e - 1, :, cols] = v[slots:]
 
             @pl.when((e == 0) & (i > 0))
             def _():
@@ -253,6 +269,12 @@
             give_back(e - 1, back - 1)
 
         in_pairs(up, e, early * (1 - (e + experts - 1) // experts), n1)
+
+        @pl.when(e == 0)
+        def _():
+            pl.semaphore_wait(free, 3)
+            send(experts - 1)
+
         in_pairs(down, e, 0, n2)
         return 0
 
@@ -261,25 +283,33 @@
         return 0
 
     lax.fori_loop(0, early, clear, 0)
-    send(experts - 1)
-    top = cell.shape[0]
-    gate = gate_ref[...].astype(jnp.bfloat16).astype(jnp.float32)
-    both = jnp.concatenate([cell.astype(jnp.float32), gate] * (4 // top), axis=0).T
-
-    def weigh(i, _):
-        c = pl.ds(pl.multiple_of(i * 256, 256), 256)
-        q = (lax.broadcasted_iota(jnp.int32, (tokens, 256), 1) + i * 256).astype(jnp.float32)
-        w = sum(jnp.where(both[:, j : j + 1] == q, both[:, top + j : top + j + 1], 0.0) for j in range(top))
-        weights[:, c] = w.astype(weights.dtype)
-        return 0
-
-    lax.fori_loop(0, weights.shape[1] // 256, weigh, 0)
     lax.fori_loop(0, starts - early // GROUP, functools.partial(start_step, False), 0)
     lax.fori_loop(starts - early // GROUP, starts, functools.partial(start_step, True), 0)
+    for q in range(CHUNKS):
+        for k in (1, 2, 3):
+            chunk_copy(q, k).wait_send()
+    for k in (1, 2, 3):
+        pl.semaphore_signal(free, inc=1, device_id=(group, peer(k)), device_id_type=MESH)
     lax.fori_loop(0, experts, expert, 0)
     give_back(experts - 1, back - 1)
 
     cells, per = members * rows_z, f // (members * rows_z)
+    top, half = cell.shape[0], DT // 2
+    gate = gate_ref[...].astype(jnp.bfloat16).astype(jnp.float32)
+    both = jnp.concatenate([cell_of(expert_ref, slot_ref, slots).astype(jnp.float32), gate] * (4 // top), axis=0).T
+    for i in range(cells // half):
+        q = (lax.broadcasted_iota(jnp.int32, (tokens, half), 1) + i * half).astype(jnp.float32)
+        w = sum(jnp.where(both[:, j : j + 1] == q, both[:, top + j : top + j + 1], 0.0) for j in range(top))
+        at = i // 2 * tokens
+        ring[3, at : at + tokens, i % 2 * half : (i % 2 + 1) * half] = w.astype(ring.dtype)
+
+    def weighted(c):
+        v = 0.0
+        for i in range(0, cells, DT):
+            n, at = min(DT, cells - i), i // DT * tokens
+            block = ring[c // per, pl.ds(pl.multiple_of(lax.rem(c, per) * cells + i, half), n), :]
+            v += jnp.dot(ring[3, at : at + tokens, :n], block, preferred_element_type=jnp.float32)
+        return v
 
     def r_copy(c, i):
         return pltpu.make_async_copy(
@@ -314,17 +344,12 @@
                 r_copy(s * PAIR + j, i).wait()
         for j in range(PAIR):
             c = s * PAIR + j
-            block = ring[c // per, pl.ds(pl.multiple_of(lax.rem(c, per) * cells, cells), cells), :]
-            v = jnp.dot(weights[...], block, preferred_element_type=jnp.float32)
-            ring[2, pl.ds(pl.multiple_of(c * tokens, tokens), tokens), :] = v.astype(ring.dtype)
+            ring[2, pl.ds(pl.multiple_of(c * tokens, tokens), tokens), :] = weighted(c).astype(ring.dtype)
         for j in range(PAIR):
             y_copy(s * PAIR + j).start()
         return 0
 
     lax.fori_loop(0, back, merge, 0)
-    for q in range(CHUNKS):
-        for k in (1, 2, 3):
-            chunk_copy(q, k).wait_send()
 
     def last(e, _):
         @pl.when(e > 0)
@@ -351,7 +376,7 @@
 def moe(expert, slot, gate, x, wg, wu, wd, members, slots):
     experts, d, f = wg.shape
     back, dma, rows = d // (DT * PAIR), pltpu.SemaphoreType.DMA, members * slots
-    n_early = GROUP * 3
+    n_early = GROUP * 4
     vmem, anywhere = pl.BlockSpec(memory_space=pltpu.VMEM), pl.BlockSpec(memory_space=pl.ANY)
     return pl.pallas_call(
         ffn_kernel,
@@ -362,12 +387,11 @@
         in_specs=[vmem] * 3 + [anywhere] * 4,
         out_specs=(anywhere, anywhere),
         scratch_shapes=[
-            pltpu.VMEM((experts, rows - slots, d), x.dtype),
+            pltpu.VMEM((experts - 1, rows - slots, d), x.dtype),
             pltpu.VMEM((experts, rows, d), x.dtype),
             pltpu.VMEM((rows, f), x.dtype),
             pltpu.VMEM((n_early, rows, 2 * FT), jnp.float32),
             pltpu.VMEM((RING, f, 2 * FT), x.dtype),
-            pltpu.VMEM((x.shape[0], members * rows), x.dtype),
             dma((d // DT,)),
             dma((RING, 2)),
             dma((experts, 3)),
@@ -379,6 +403,7 @@
             dma((experts, back)),
             dma((d // DT, members)),
             dma((d // DT,)),
+            pltpu.SemaphoreType.REGULAR,
         ],
         compiler_params=pltpu.CompilerParams(
             collective_id=0, has_side_effects=True, vmem_limit_bytes=67_000_000

time: 272 us -> 268 us (0.985)
  Pallas kernels: 267 us -> 263 us
    pallas_call x1, Pallas kernels: 267 us -> 263 us  [moe(): pl.pallas_call(ffn_kernel, out_shape=(jax.ShapeDtypeStruct(x.shape, x.dty...]
where the time goes in v5:
time: 268 us
  Pallas kernels  263 us (98%)
  local copies, waits for them, and re-layouts  4.7 us (2%)
    pallas_call x1, Pallas kernels, moe(): pl.pallas_call(ffn_kernel, out_shape=(jax.ShapeDtypeStruct(x.shape, x.dty...  263 us

profile of v5, /device:TPU:0, one launch (start us, length us, event | category | flops | bytes accessed | tf_op | source)
XLA Modules:
  0.0 267.9 jit_solution(3987785076711732507)
XLA Ops:
  0.0 263.2 %shard_map.73 = (bf16[512,4096]{1,0:T(8,128)(2,1)}, bf16[4,320,4096]{2,1,0:T(8,128)(2,1)}) custom-call(s32[2,512]{1,0:T(2,128)} %bitcast.13, s32[2,512]{1,0:T(2,128)} %bitcast.14, f32[2,512]{1,0:T(2,128)} %bitcast.15, bf16[512,4096]{1,0:T(8,128)(2,1)} %bitcast.11, bf16[4,4096,6400]{2,1,0:T(8,128)(2,1)} %wg.1, bf16[4,4096,6400]{2,1,0:T(8,128)(2,1)} %wu.1, ...), custom_call_target="tpu_custom_call" | custom-call | tf_op jit(solution)/shard_map/pallas_call | solution.py:381
  263.2 4.7 %copy.9 = bf16[1,1,512,4096]{3,2,1,0:T(8,128)(2,1)} copy(bf16[1,1,512,4096]{3,2,1,0:T(8,128)(2,1)} %bitcast.12) | data formatting | bytes 8388608
